TPU v7x, 32 devices: a whole 2x2x4 slice. The times are simulated.
32 devices in a mesh: grp: 4 (over y, x), seq: 8 (over z, core).
Axes of the slice: x: 2, y: 2, z: 4, core: 2. Of those that a mesh axis runs over, the one named last changes fastest.
Arguments:
- queries: bfloat16 [8192, 2048], P(('grp', 'seq')), may hold values from -48 to 48
- key_rows: bfloat16 [8192, 512], P(('grp', 'seq')), may hold values from -4.5 to 4.5
- value_rows: bfloat16 [8192, 512], P(('grp', 'seq')), may hold values from -6 to 6
- segments: int32 [8192], P(('grp', 'seq')), may hold values from 0 to 3, as said below
Outputs:
- attended: bfloat16 [8192, 2048], P(('grp', 'seq'))
- log_sums: float32 [16, 8192], P(None, ('grp', 'seq'))
Inputs may be any that keep to these rules, and one draw needn't show every extreme that they name: `segments`: never falls along the sequence, starts at 0 and rises by one at each new document; the last token holds the largest value.
All inputs are finite; a program needn't handle non-finite values.
Results may differ from a plain program's by a relative error of at most 0.0035.
Values may be sent and summed in bfloat16 or wider, within the bound.
A program may use at most 192 MiB of HBM per device.

v0:
```python
import math

import jax
import jax.numpy as jnp
from jax import lax
from jax.experimental import pallas as pl
from jax.experimental.pallas import tpu as pltpu
from jax.sharding import PartitionSpec as P

Q_HEADS = 16
KV_HEADS = 4
HEAD_DIM = 128
WINDOW = 4096
AXES = ("grp", "seq")
LOW = -1e30


def head_step(h, qt, k_ref, vt, m_ref, l_ref, acc, bias):
    c = math.log2(math.e) / math.sqrt(HEAD_DIM)
    g = h // (Q_HEADS // KV_HEADS)
    s = jnp.dot(k_ref[:, g * HEAD_DIM : (g + 1) * HEAD_DIM], qt[h], preferred_element_type=jnp.float32)
    if bias is not None:
        s = s + bias[...]
    m_old = m_ref[h]
    m_new = jnp.maximum(m_old, jnp.max(s, axis=0, keepdims=True))
    p = jnp.exp2((s - m_new) * c)
    alpha = jnp.exp2((m_old - m_new) * c)
    l_ref[h] = l_ref[h] * alpha + jnp.sum(p, axis=0, keepdims=True)
    m_ref[h] = m_new
    acc[h] = acc[h] * alpha + jnp.dot(vt, p.astype(jnp.bfloat16), preferred_element_type=jnp.float32)


def block_step(qt, k_ref, v_ref, m_ref, l_ref, acc, bias):
    group = Q_HEADS // KV_HEADS
    for g in range(KV_HEADS):
        vt = v_ref[:, g * HEAD_DIM : (g + 1) * HEAD_DIM].T
        for h in range(g * group, (g + 1) * group):
            head_step(h, qt, k_ref, vt, m_ref, l_ref, acc, bias)


def flash(info, lower_ref, q_ref, k_ref, v_ref, o_ref, ls_ref, qt, m_ref, l_ref, acc, bias):
    j = pl.program_id(0)
    tok = q_ref.shape[0]
    device, first, clean = info[0], info[1], info[2]

    @pl.when(j == 0)
    def _():
        for h in range(Q_HEADS):
            qt[h] = q_ref[:, h * HEAD_DIM : (h + 1) * HEAD_DIM].T
        m_ref[...] = jnp.full_like(m_ref, LOW)
        l_ref[...] = jnp.zeros_like(l_ref)
        acc[...] = jnp.zeros_like(acc)

    block = device - j
    edge = (j == 0) | (block < clean)

    @pl.when((block >= first) & edge)
    def _():
        key_pos = block * tok + lax.broadcasted_iota(jnp.int32, (tok, tok), 0)
        pos = device * tok + lax.broadcasted_iota(jnp.int32, (tok, tok), 1)
        allowed = (key_pos >= lower_ref[...]) & (key_pos <= pos)
        bias[...] = jnp.where(allowed, 0.0, LOW)
        block_step(qt, k_ref, v_ref, m_ref, l_ref, acc, bias)

    @pl.when((block >= first) & jnp.logical_not(edge))
    def _():
        block_step(qt, k_ref, v_ref, m_ref, l_ref, acc, None)

    @pl.when(j == pl.num_programs(0) - 1)
    def _():
        for h in range(Q_HEADS):
            out = acc[h] * (1.0 / l_ref[h])
            o_ref[:, h * HEAD_DIM : (h + 1) * HEAD_DIM] = out.T.astype(o_ref.dtype)
            ls_ref[h : h + 1, :] = m_ref[h] * (1.0 / math.sqrt(HEAD_DIM)) + jnp.log(l_ref[h])


def on_device(queries, key_rows, value_rows, segments):
    tok = queries.shape[0]
    width = key_rows.shape[1]
    device = lax.axis_index(AXES)
    k_all = lax.all_gather(key_rows, AXES, tiled=True)
    v_all = lax.all_gather(value_rows, AXES, tiled=True)
    seg_all = lax.all_gather(segments, AXES, tiled=True)
    starts = jnp.sum((seg_all[:, None] < segments[None, :]).astype(jnp.int32), axis=0)
    positions = device * tok + jnp.arange(tok, dtype=jnp.int32)
    lower = jnp.maximum(starts, positions - WINDOW + 1)
    first = jnp.min(lower) // tok
    clean = (jnp.max(lower) + tok - 1) // tok
    info = jnp.stack([device, first, clean]).astype(jnp.int32)
    reach = (WINDOW - 1 + tok - 1) // tok + 1

    def kv_index(j, info):
        return (jnp.maximum(info[0] - j, info[1]), 0)

    const = lambda j, info: (0, 0)
    return pl.pallas_call(
        flash,
        grid_spec=pltpu.PrefetchScalarGridSpec(
            num_scalar_prefetch=1,
            grid=(reach,),
            in_specs=[
                pl.BlockSpec((1, tok), const),
                pl.BlockSpec(queries.shape, const),
                pl.BlockSpec((tok, width), kv_index),
                pl.BlockSpec((tok, width), kv_index),
            ],
            out_specs=[
                pl.BlockSpec(queries.shape, const),
                pl.BlockSpec((Q_HEADS, tok), const),
            ],
            scratch_shapes=[
                pltpu.VMEM((Q_HEADS, HEAD_DIM, tok), jnp.bfloat16),
                pltpu.VMEM((Q_HEADS, 1, tok), jnp.float32),
                pltpu.VMEM((Q_HEADS, 1, tok), jnp.float32),
                pltpu.VMEM((Q_HEADS, HEAD_DIM, tok), jnp.float32),
                pltpu.VMEM((tok, tok), jnp.float32),
            ],
        ),
        out_shape=[
            jax.ShapeDtypeStruct(queries.shape, jnp.bfloat16),
            jax.ShapeDtypeStruct((Q_HEADS, tok), jnp.float32),
        ],
        compiler_params=pltpu.CompilerParams(dimension_semantics=("arbitrary",)),
    )(info, lower[None, :], queries, k_all, v_all)


def solution(mesh):
    in_specs = (P(AXES, None), P(AXES, None), P(AXES, None), P(AXES))
    out_specs = (P(AXES, None), P(None, AXES))
    return jax.shard_map(
        on_device, mesh=mesh, in_specs=in_specs, out_specs=out_specs, check_vma=False
    )
```

profile of v0, /device:TPU:31, one launch (start us, length us, event | category | flops | bytes accessed | tf_op | source)
XLA Modules:
  0.0 250.4 jit_solution(6450287693878540349)
XLA Ops:
  7.2 0.0 all-gather.4.cloned.1.call-start
  7.2 0.7 all-gather.4.cloned.1.call-update
  7.9 0.0 all-gather.6.cloned.1.call-start
  7.9 0.7 all-gather.6.cloned.1.call-update
  8.7 36.6 %all-gather = s32[32,1,256]{2,1,0:T(1,128)S(1)} all-gather(s32[1,1,256]{2,1,0:T(1,128)} %bitcast.8), channel_id=1, replica_groups=mesh['grp'=4,'seq'=8] {'grp','seq'}, dimensions={0}, use_global_device_ids=true | all-gather | bytes 33792 | tf_op jit(solution)/shard_map/all_gather | solution.py:83
  45.2 4.4 %convert_reduce_fusion = s32[256]{0:T(256)S(1)} fusion(s32[256]{0:T(256)} %param.7, s32[8192]{0:T(1024)S(1)} %bitcast.6), kind=kLoop, calls=%fused_computation | loop fusion | flops 6291200 | bytes 34816 | tf_op jit(solution)/shard_map/reduce_sum | solution.py:84
  49.6 0.6 fusion.1
  53.4 0.7 pad_add_fusion.info
  54.1 0.6 add_maximum_fusion.lower_ref
  54.7 32.4 %all-gather.4.cloned.1.call-done.k_ref = bf16[8192,512]{1,0:T(8,128)(2,1)} async-done(((bf16[256,512]{1,0:T(8,128)(2,1)}), bf16[8192,512]{1,0:T(8,128)(2,1)}) %all-gather.4.cloned.1.call-update) | async-done | bytes 8388624 | tf_op jit(solution)/shard_map/all_gather | solution.py:81
  87.1 78.7 %all-gather.6.cloned.1.call-done.v_ref = bf16[8192,512]{1,0:T(8,128)(2,1)} async-done(((bf16[256,512]{1,0:T(8,128)(2,1)}), bf16[8192,512]{1,0:T(8,128)(2,1)}) %all-gather.6.cloned.1.call-update) | async-done | bytes 8388624 | tf_op jit(solution)/shard_map/all_gather | solution.py:82
  165.8 77.7 %shard_map.59 = (bf16[256,2048]{1,0:T(8,128)(2,1)}, f32[16,256]{1,0:T(8,128)}) custom-call(s32[3]{0:T(128)} %pad_add_fusion.info, s32[1,256]{1,0:T(1,128)} %add_maximum_fusion.lower_ref, bf16[256,2048]{1,0:T(8,128)(2,1)} %q_ref.1, bf16[8192,512]{1,0:T(8,128)(2,1)} %all-gather.4.cloned.1.call-done.k_ref, bf16[8192,512]{1,0:T(8,128)(2,1)} %all-gather.6.cloned.1.call-done.v_ref), custom_call_target="tpu_custom_call" | custom-call | tf_op jit(solution)/shard_map/pallas_call | solution.py:96
Async XLA Ops:
  7.2 80.0 %all-gather.4.cloned.1.call-start = ((), (), s32[]{:S(2)}) async-start(), calls=%async_computation | async-start | bytes 8650752 | tf_op jit(solution)/shard_map/all_gather | solution.py:81
  7.9 157.9 %all-gather.6.cloned.1.call-start = ((), (), s32[]{:S(2)}) async-start(), calls=%async_computation.1 | async-start | bytes 8650752 | tf_op jit(solution)/shard_map/all_gather | solution.py:82
Sparse Core Ops, SparseCore 0:
  11.0 76.1 all-gather.3
  90.1 75.6 all-gather.5
where the time goes:
time: 251 us; the launch traced here: 250 us
  waiting for transfers between devices  113 us (45%)
  Pallas kernels  77.7 us (31%)
  blocking collectives  36.6 us (15%)
  between operations  17.2 us (7%)
  other arithmetic  6.28 us (3%)
    all_gather x1, waiting for transfers between devices, on_device(): v_all = lax.all_gather(value_rows, AXES, tiled=True)  78.7 us
    pallas_call x1, Pallas kernels, on_device(): pl.pallas_call(flash, grid_spec=pltpu.PrefetchScalarGridSpec(num_scalar_p...  77.7 us
    all_gather x1, blocking collectives, on_device(): seg_all = lax.all_gather(segments, AXES, tiled=True)  36.6 us
    all_gather x1, waiting for transfers between devices, on_device(): k_all = lax.all_gather(key_rows, AXES, tiled=True)  32.4 us
  transfers between devices with their start and end apart: 2, of which 2 were waited for; matrix products, arithmetic and copies ran while one was open for 3% of the time, Pallas kernels for 0%

commit v1 on v0

--- a/solution.py
+++ b/solution.py
@@ -1,3 +1,4 @@
+import functools
 import math
 
 import jax
@@ -74,23 +75,192 @@
             ls_ref[h : h + 1, :] = m_ref[h] * (1.0 / math.sqrt(HEAD_DIM)) + jnp.log(l_ref[h])
 
 
+def spread(grp_n, k_in, v_in, s_in, k_out, v_out, s_out, send, recv, own):
+    seq_n = k_out.shape[0] // 3
+    chips = seq_n // 2
+    c, s = lax.axis_index("grp"), lax.axis_index("seq")
+    z, core = s // 2, s % 2
+    even = c % 2 == 0
+    srcs, bufs = (k_in, v_in, s_in), (k_out, v_out, s_out)
+    sib = s + 1 - 2 * core
+    pair = c + 1 - 2 * (c % 2)
+    peers = (
+        (z + 1 < chips, (c, s + 2)),
+        (z > 0, (c, s - 2)),
+        (c >= 0, (pair, s)),
+        (c + 2 < grp_n, (c + 2, s)),
+        (c >= 2, (c - 2, s)),
+        (c >= 0, (c, sib)),
+    )
+    barrier = pltpu.get_barrier_semaphore()
+    count = 0
+    for ok, to in peers:
+        count = count + ok.astype(jnp.int32)
+
+        @pl.when(ok)
+        def _(to=to):
+            pl.semaphore_signal(barrier, inc=1, device_id=to, device_id_type=pl.DeviceIdType.MESH)
+
+    pl.semaphore_wait(barrier, count)
+
+    def slot(dc, zz, cc):
+        return (2 - dc) * seq_n + 2 * zz + cc
+
+    def copy(t, kind, zz, src_slot, dst_slot, to, source=None):
+        src = bufs[t].at[src_slot] if source is None else source
+        return pltpu.make_async_remote_copy(
+            src_ref=src,
+            dst_ref=bufs[t].at[dst_slot],
+            send_sem=send.at[kind, zz, t],
+            recv_sem=recv.at[dst_slot, t],
+            device_id=to,
+            device_id_type=pl.DeviceIdType.MESH,
+        )
+
+    def sends(dc, zz, t, act, mine=False):
+        here = slot(dc, zz, core)
+        source = srcs[t] if mine else None
+
+        def go(ok, kind, dst, to):
+            @pl.when(ok)
+            def _():
+                act(copy(t, kind, zz, here, dst, to, source))
+
+        if dc == 0:
+            go((zz <= z) & (z + 1 < chips), 0, here, (c, s + 2))
+            go((zz >= z) & (z > 0), 1, here, (c, s - 2))
+            go((c + 2 < grp_n) & (jnp.logical_not(even) | (zz >= z)), 3, slot(2, zz, core), (c + 2, s))
+            go(even, 2, slot(1, zz, core), (c + 1, s))
+            go(zz <= z, 4, here, (c, sib))
+        elif dc == 1:
+            go(zz >= 0, 5, here, (c, sib))
+        else:
+            go(jnp.logical_not(even), 7, slot(1, zz, core), (c - 1, s))
+            go(zz >= z, 6, here, (c, sib))
+
+    def present(dc, zz):
+        inside = (zz >= 0) & (zz < chips)
+        if dc == 0:
+            return inside
+        if dc == 1:
+            return inside & (c >= 1)
+        return inside & (c >= 2) & (jnp.logical_not(even) | (zz >= z))
+
+    def arrived(dc, zz, cc, t):
+        here = slot(dc, zz, cc)
+        pltpu.make_async_remote_copy(
+            src_ref=bufs[t].at[here],
+            dst_ref=bufs[t].at[here],
+            send_sem=send.at[0, 0, t],
+            recv_sem=recv.at[here, t],
+            device_id=(c, sib),
+            device_id_type=pl.DeviceIdType.MESH,
+        ).wait_recv()
+
+    def local(t):
+        return pltpu.make_async_copy(srcs[t], bufs[t].at[slot(0, z, core)], own.at[t])
+
+    for t in range(3):
+        sends(0, z, t, lambda d: d.start(), True)
+    for t in range(3):
+        local(t).start()
+
+    def event(dc, zz):
+        @pl.when(present(dc, zz))
+        def _():
+            for t in range(3):
+                arrived(dc, zz, core, t)
+                sends(dc, zz, t, lambda d: d.start())
+
+    for r in range(1, chips + 1):
+        if r < chips:
+            event(0, z - r)
+            event(0, z + r)
+        for sign in (-1, 1) if r > 1 else (1,):
+            event(2, z + sign * (r - 1))
+            event(1, z + sign * (r - 1))
+
+    for zz in range(chips):
+        for dc in range(3):
+            zv = zz + 0 * z
+
+            def finish(dc=dc, zv=zv):
+                for t in range(3):
+                    sends(dc, zv, t, lambda d: d.wait_send())
+
+            if dc == 0:
+                finish()
+            else:
+                pl.when(present(dc, zv))(finish)
+            theirs = (zv <= z) if dc == 0 else (c >= 1) if dc == 1 else (c >= 2) & (zv >= z)
+
+            @pl.when(theirs)
+            def _(dc=dc, zv=zv):
+                for t in range(3):
+                    arrived(dc, zv, 1 - core, t)
+
+    for t in range(3):
+        local(t).wait()
+
+
+def gather_rows(key_rows, value_rows, segments):
+    grp_n, seq_n = lax.axis_size("grp"), lax.axis_size("seq")
+    tok, width = key_rows.shape
+    hbm = pl.BlockSpec(memory_space=pl.ANY)
+    slots = 3 * seq_n
+    return pl.pallas_call(
+        functools.partial(spread, grp_n),
+        out_shape=[
+            jax.ShapeDtypeStruct((slots, tok, width), jnp.bfloat16),
+            jax.ShapeDtypeStruct((slots, tok, width), jnp.bfloat16),
+            jax.ShapeDtypeStruct((slots, 1, tok), jnp.int32),
+        ],
+        in_specs=[hbm] * 3,
+        out_specs=[hbm] * 3,
+        scratch_shapes=[
+            pltpu.SemaphoreType.DMA((8, seq_n // 2, 3)),
+            pltpu.SemaphoreType.DMA((slots, 3)),
+            pltpu.SemaphoreType.DMA((3,)),
+        ],
+        compiler_params=pltpu.CompilerParams(collective_id=0, has_side_effects=True),
+    )(key_rows, value_rows, segments[None, :])
+
+
 def on_device(queries, key_rows, value_rows, segments):
     tok = queries.shape[0]
-    width = key_rows.shape[1]
+    grp_n, seq_n = lax.axis_size("grp"), lax.axis_size("seq")
     device = lax.axis_index(AXES)
-    k_all = lax.all_gather(key_rows, AXES, tiled=True)
-    v_all = lax.all_gather(value_rows, AXES, tiled=True)
-    seg_all = lax.all_gather(segments, AXES, tiled=True)
-    starts = jnp.sum((seg_all[:, None] < segments[None, :]).astype(jnp.int32), axis=0)
-    positions = device * tok + jnp.arange(tok, dtype=jnp.int32)
+    offset = device * tok
+    if 2 * seq_n * tok == WINDOW and grp_n % 2 == 0 and seq_n % 2 == 0:
+        k_all, v_all, seg_all = gather_rows(key_rows, value_rows, segments)
+        base = (lax.axis_index("grp") - 2) * seq_n
+    else:
+        k_all = lax.all_gather(key_rows, AXES)
+        v_all = lax.all_gather(value_rows, AXES)
+        seg_all = lax.all_gather(segments, AXES)
+        base = 0
+    seg_all = seg_all.reshape(-1)
+    key_pos = base * tok + jnp.arange(seg_all.shape[0], dtype=jnp.int32)
+    begin = jnp.maximum(offset - WINDOW, 0)
+    before = (key_pos >= begin) & (key_pos < offset) & (seg_all < segments[0])
+    carried = begin + jnp.sum(before.astype(jnp.int32))
+    inner = jnp.sum((segments[:, None] < segments[None, :]).astype(jnp.int32), axis=0)
+    starts = jnp.where(segments == segments[0], carried, offset + inner)
+    positions = offset + jnp.arange(tok, dtype=jnp.int32)
     lower = jnp.maximum(starts, positions - WINDOW + 1)
     first = jnp.min(lower) // tok
     clean = (jnp.max(lower) + tok - 1) // tok
-    info = jnp.stack([device, first, clean]).astype(jnp.int32)
+    info = jnp.stack([device, first, clean, device - base]).astype(jnp.int32)
     reach = (WINDOW - 1 + tok - 1) // tok + 1
+    return attention(info, lower, queries, k_all, v_all, reach)
+
+
+def attention(info, lower, queries, k_all, v_all, reach):
+    tok = queries.shape[0]
+    width = k_all.shape[2]
 
     def kv_index(j, info):
-        return (jnp.maximum(info[0] - j, info[1]), 0)
+        return (jnp.maximum(info[3] - j, info[3] - info[0] + info[1]), 0, 0)
 
     const = lambda j, info: (0, 0)
     return pl.pallas_call(
@@ -101,8 +271,8 @@
             in_specs=[
                 pl.BlockSpec((1, tok), const),
                 pl.BlockSpec(queries.shape, const),
-                pl.BlockSpec((tok, width), kv_index),
-                pl.BlockSpec((tok, width), kv_index),
+                pl.BlockSpec((None, tok, width), kv_index),
+                pl.BlockSpec((None, tok, width), kv_index),
             ],
             out_specs=[
                 pl.BlockSpec(queries.shape, const),

time: 251 us -> 149 us (0.59)
  waiting for transfers between devices: 113 us -> 0 us
  Pallas kernels: 77.7 us -> 137 us
  blocking collectives: 36.6 us -> 0 us
  between operations: 17.2 us -> 4.77 us
    all_gather x2 -> x0, waiting for transfers between devices: 111 us -> none  [the longest x1 78.7 us: on_device(): v_all = lax.all_gather(value_rows, AXES, tiled=True)]
    pallas_call x1 -> x2, Pallas kernels: 77.7 us -> 137 us  [the longest x1 77.7 us: attention(): pl.pallas_call(flash, grid_spec=pltpu.PrefetchScalarGridSpec(num_scalar_p...]
    all_gather x1 -> x0, blocking collectives: 36.6 us -> none  [on_device(): seg_all = lax.all_gather(segments, AXES, tiled=True)]
  transfers between devices with their start and end apart: 2 -> 0, of which waited for: 2 -> 0; matrix products, arithmetic and copies ran while one was open for 3% -> 0% of each run, Pallas kernels for 0% -> 0%
where the time goes in v1:
time: 149 us
  Pallas kernels  137 us (92%)
  other arithmetic  6.24 us (4%)
  between operations  4.77 us (3%)
    pallas_call x1, Pallas kernels, attention(): pl.pallas_call(flash, grid_spec=pltpu.PrefetchScalarGridSpec(num_scalar_p...  77.7 us
    pallas_call x1, Pallas kernels, gather_rows(): pl.pallas_call(functools.partial(spread, grp_n), out_shape=[jax.ShapeDtyp...  59 us

profile of v1, /device:TPU:31, one launch (start us, length us, event | category | flops | bytes accessed | tf_op | source)
XLA Modules:
  0.0 149.0 jit_solution(14420795859205333624)
XLA Ops:
  0.6 1.3 slice.4
  1.9 0.9 convert_reduce_fusion
  2.8 59.0 %shard_map.59 = (bf16[24,256,512]{2,1,0:T(8,128)(2,1)}, bf16[24,256,512]{2,1,0:T(8,128)(2,1)}, s32[24,1,256]{2,1,0:T(1,128)}) custom-call(bf16[256,512]{1,0:T(8,128)(2,1)} %k_in.1, bf16[256,512]{1,0:T(8,128)(2,1)} %v_in.1, s32[1,256]{1,0:T(1,128)} %bitcast.7), custom_call_target="tpu_custom_call" | custom-call | tf_op jit(solution)/shard_map/pallas_call | solution.py:211
  61.8 2.1 %fusion = s32[]{:T(128)} fusion(s32[24,1,256]{2,1,0:T(1,128)} %get-tuple-element.5, s32[]{:T(128)} %bitcast.1, s32[]{:T(128)S(6)} %mul.13, s32[]{:T(128)S(6)} %max.6, s32[]{:T(128)S(6)} %mul.14), kind=kLoop, calls=%fused_computation.2 | loop fusion | flops 61439 | bytes 24596 | tf_op jit(solution)/shard_map/reduce_sum | solution.py:246
  64.6 2.6 %fusion.2 = (s32[]{:T(128)}, s32[]{:T(128)}, s32[256]{0:T(256)}) fusion(s32[256]{0:T(256)S(1)} %convert_reduce_fusion, s32[]{:T(128)S(6)} %mul.13, s32[]{:T(128)S(6)} %add.57, s32[256]{0:T(256)} %param.7, s32[]{:T(128)} %bitcast.1), kind=kLoop, calls=%fused_computation.6 | loop fusion | flops 2046 | bytes 3092 | tf_op jit(solution)/shard_map/reduce_min | solution.py:251
  70.6 0.7 pad_add_fusion.info
  71.3 77.7 %shard_map.60 = (bf16[256,2048]{1,0:T(8,128)(2,1)}, f32[16,256]{1,0:T(8,128)}) custom-call(s32[4]{0:T(128)} %pad_add_fusion.info, s32[1,256]{1,0:T(1,128)} %bitcast.8, bf16[256,2048]{1,0:T(8,128)(2,1)} %q_ref.1, bf16[24,256,512]{2,1,0:T(8,128)(2,1)} %get-tuple-element.6.k_ref, bf16[24,256,512]{2,1,0:T(8,128)(2,1)} %get-tuple-element.7.v_ref), custom_call_target="tpu_custom_call" | custom-call | tf_op jit(solution)/shard_map/pallas_call | solution.py:266

commit v2 on v1

--- a/solution.py
+++ b/solution.py
@@ -16,27 +16,42 @@
 LOW = -1e30
 
 
-def head_step(h, qt, k_ref, vt, m_ref, l_ref, acc, bias):
+def block_step(qt, k_ref, v_ref, m_ref, l_ref, acc, bias):
     c = math.log2(math.e) / math.sqrt(HEAD_DIM)
-    g = h // (Q_HEADS // KV_HEADS)
-    s = jnp.dot(k_ref[:, g * HEAD_DIM : (g + 1) * HEAD_DIM], qt[h], preferred_element_type=jnp.float32)
-    if bias is not None:
-        s = s + bias[...]
-    m_old = m_ref[h]
-    m_new = jnp.maximum(m_old, jnp.max(s, axis=0, keepdims=True))
-    p = jnp.exp2((s - m_new) * c)
-    alpha = jnp.exp2((m_old - m_new) * c)
-    l_ref[h] = l_ref[h] * alpha + jnp.sum(p, axis=0, keepdims=True)
-    m_ref[h] = m_new
-    acc[h] = acc[h] * alpha + jnp.dot(vt, p.astype(jnp.bfloat16), preferred_element_type=jnp.float32)
-
-
-def block_step(qt, k_ref, v_ref, m_ref, l_ref, acc, bias):
     group = Q_HEADS // KV_HEADS
-    for g in range(KV_HEADS):
-        vt = v_ref[:, g * HEAD_DIM : (g + 1) * HEAD_DIM].T
-        for h in range(g * group, (g + 1) * group):
-            head_step(h, qt, k_ref, vt, m_ref, l_ref, acc, bias)
+
+    def scores(h):
+        g = h // group
+        return jnp.dot(
+            k_ref[:, g * HEAD_DIM : (g + 1) * HEAD_DIM], qt[h], preferred_element_type=jnp.float32
+        )
+
+    def summed(h, p, alpha):
+        g = h // group
+        if h % group == 0:
+            vts[g] = v_ref[:, g * HEAD_DIM : (g + 1) * HEAD_DIM].T
+        acc[h] = acc[h] * alpha + jnp.dot(vts[g], p, preferred_element_type=jnp.float32)
+
+    vts = {}
+    AHEAD = 2
+    ready = [scores(h) for h in range(AHEAD)]
+    waiting = None
+    for h in range(Q_HEADS):
+        if h + AHEAD < Q_HEADS:
+            ready.append(scores(h + AHEAD))
+        s = ready.pop(0)
+        if bias is not None:
+            s = s + bias[...]
+        m_old = m_ref[h]
+        m_new = jnp.maximum(m_old, jnp.max(s, axis=0, keepdims=True))
+        p = jnp.exp2((s - m_new) * c)
+        alpha = jnp.exp2((m_old - m_new) * c)
+        l_ref[h] = l_ref[h] * alpha + jnp.sum(p, axis=0, keepdims=True)
+        m_ref[h] = m_new
+        if waiting is not None:
+            summed(*waiting)
+        waiting = (h, p.astype(jnp.bfloat16), alpha)
+    summed(*waiting)
 
 
 def flash(info, lower_ref, q_ref, k_ref, v_ref, o_ref, ls_ref, qt, m_ref, l_ref, acc, bias):

time: 149 us -> 106 us (0.71)
  Pallas kernels: 137 us -> 93.4 us
    pallas_call x1, Pallas kernels: 77.7 us -> 34.4 us  [attention(): pl.pallas_call(flash, grid_spec=pltpu.PrefetchScalarGridSpec(num_scalar_p...]
where the time goes in v2:
time: 106 us
  Pallas kernels  93.4 us (88%)
  other arithmetic  6.24 us (6%)
  between operations  4.77 us (4%)
  local copies, waits for them, and re-layouts  1.26 us (1%)
    pallas_call x1, Pallas kernels, gather_rows(): pl.pallas_call(functools.partial(spread, grp_n), out_shape=[jax.ShapeDtyp...  59 us
    pallas_call x1, Pallas kernels, attention(): pl.pallas_call(flash, grid_spec=pltpu.PrefetchScalarGridSpec(num_scalar_p...  34.4 us
    reduce_min x1, other arithmetic, on_device(): first = jnp.min(lower) // tok  2.59 us
    reduce_sum x1, other arithmetic, on_device(): carried = begin + jnp.sum(before.astype(jnp.int32))  2.13 us

profile of v2, /device:TPU:31, one launch (start us, length us, event | category | flops | bytes accessed | tf_op | source)
XLA Modules:
  0.0 105.6 jit_solution(531331517532578622)
XLA Ops:
  0.6 1.3 %slice.4 = s32[1]{0:T(128)} slice(s32[256]{0:T(256)} %param.7), slice={[0:1]} | slice | bytes 8 | tf_op jit(solution)/shard_map/slice | solution.py:263
  1.9 0.9 convert_reduce_fusion
  2.8 59.0 %shard_map.59 = (bf16[24,256,512]{2,1,0:T(8,128)(2,1)}, bf16[24,256,512]{2,1,0:T(8,128)(2,1)}, s32[24,1,256]{2,1,0:T(1,128)}) custom-call(bf16[256,512]{1,0:T(8,128)(2,1)} %k_in.1, bf16[256,512]{1,0:T(8,128)(2,1)} %v_in.1, s32[1,256]{1,0:T(1,128)} %bitcast.7), custom_call_target="tpu_custom_call" | custom-call | tf_op jit(solution)/shard_map/pallas_call | solution.py:226
  61.8 2.1 %fusion = s32[]{:T(128)} fusion(s32[24,1,256]{2,1,0:T(1,128)} %get-tuple-element.5, s32[]{:T(128)} %bitcast.1, s32[]{:T(128)S(6)} %mul.13, s32[]{:T(128)S(6)} %max.6, s32[]{:T(128)S(6)} %mul.14), kind=kLoop, calls=%fused_computation.2 | loop fusion | flops 61439 | bytes 24596 | tf_op jit(solution)/shard_map/reduce_sum | solution.py:261
  64.6 2.6 %fusion.2 = (s32[]{:T(128)}, s32[]{:T(128)}, s32[256]{0:T(256)}) fusion(s32[256]{0:T(256)S(1)} %convert_reduce_fusion, s32[]{:T(128)S(6)} %mul.13, s32[]{:T(128)S(6)} %add.57, s32[256]{0:T(256)} %param.7, s32[]{:T(128)} %bitcast.1), kind=kLoop, calls=%fused_computation.6 | loop fusion | flops 2046 | bytes 3092 | tf_op jit(solution)/shard_map/reduce_min | solution.py:266
  70.6 0.7 pad_add_fusion.info
  71.3 34.4 %shard_map.60 = (bf16[256,2048]{1,0:T(8,128)(2,1)}, f32[16,256]{1,0:T(8,128)}) custom-call(s32[4]{0:T(128)} %pad_add_fusion.info, s32[1,256]{1,0:T(1,128)} %bitcast.8, bf16[256,2048]{1,0:T(8,128)(2,1)} %q_ref.1, bf16[24,256,512]{2,1,0:T(8,128)(2,1)} %get-tuple-element.6.k_ref, bf16[24,256,512]{2,1,0:T(8,128)(2,1)} %get-tuple-element.7.v_ref), custom_call_target="tpu_custom_call" | custom-call | tf_op jit(solution)/shard_map/pallas_call | solution.py:281
